TPU v7x, 32 devices: a whole 2x2x4 slice. The times are simulated.
32 devices in a mesh: row: 8 (over z, y), col: 4 (over x, core).
Axes of the slice: x: 2, y: 2, z: 4, core: 2. Of those that a mesh axis runs over, the one named last changes fastest.
Arguments:
- tile_seeds: int32 [32, 8, 64, 4], P(None, 'row', None, 'col'), may hold values from 0 to 1073741823
- factors: bfloat16 [32, 1024, 64, 512], P(None, 'row', None, 'col'), may hold values from -0.015625 to 0.015625
- lower_inverse: bfloat16 [4, 16, 512, 8, 1024], P(None, None, 'col', None, 'row'), may hold values from -0.1 to 2
- upper_inverse: bfloat16 [4, 16, 512, 8, 1024], P(None, None, 'col', None, 'row'), may hold values from -0.1 to 2
- right_side: float32 [32, 1024], P(None, 'row'), may hold values from -6 to 6
- first_guess: float32 [64, 512], P(None, 'col'), may hold values from -6 to 6
Outputs:
- solution: float32 [64, 512], P(None, 'col')
- hessenberg: float32 [4, 3], replicated
All inputs are finite; a program needn't handle non-finite values.
Results may differ from a plain program's by a relative error of at most 0.011.
Values may be sent and summed in bfloat16 or wider, within the bound.
No kernel may reach another device: no remote copies, remote signals or barrier semaphores. Data moves between devices by JAX's collectives and lax.ppermute only.
A program may use at most 320 MiB of HBM per device.

v0:
```python
import jax
import jax.numpy as jnp
from jax import lax
from jax.sharding import PartitionSpec as P

ORDER = 32768
SWEEPS = 4
ITERS = 3
DIAG_ORDER = 8192
DIAG_SHIFT = 2.0


def scrambled(tile_seed, flat_index):
    hashed = tile_seed + flat_index * 1640531527
    hashed = hashed ^ hashed >> 16 & 65535
    hashed = hashed * 2146121005
    hashed = hashed ^ hashed >> 15 & 131071
    hashed = hashed * 1779033703
    hashed = hashed ^ hashed >> 16 & 65535
    high_bits = hashed >> 8 & 16777215
    return (high_bits.astype(jnp.float32) - 8388607.5) / 8388608.0


def small_solve(normal_matrix, target):
    factor = jnp.linalg.cholesky(normal_matrix)
    order_small = normal_matrix.shape[0]
    forward = []
    for position in range(order_small):
        partial_value = target[position]
        for earlier in range(position):
            partial_value = partial_value - factor[position, earlier] * forward[earlier]
        forward.append(partial_value / factor[position, position])
    backward = [None] * order_small
    for position in reversed(range(order_small)):
        partial_value = forward[position]
        for after_pos in range(position + 1, order_small):
            partial_value = partial_value - factor[after_pos, position] * backward[after_pos]
        backward[position] = partial_value / factor[position, position]
    return backward


def matrix_part(seed_grid, vector_col, row_index, col_index, n_row, n_col):
    tile_size = vector_col.shape[1]
    offsets = jnp.arange(tile_size, dtype=jnp.int32)
    flat_index = offsets[:, None] * tile_size + offsets[None, :]
    col_tiles = jnp.arange(seed_grid.shape[1], dtype=jnp.int32)
    col_ids = (col_tiles[:, None] * n_col + col_index) * tile_size + offsets[None, :]
    entry_scale = ORDER ** (-0.5)

    def one_row(inputs):
        seed_row, tile_row = inputs
        values = scrambled(seed_row[None, :, None], flat_index[:, None, :]) * entry_scale
        row_ids = (tile_row * n_row + row_index) * tile_size + offsets
        values = values + jnp.where(row_ids[:, None, None] == col_ids[None, :, :], DIAG_SHIFT, 0.0)
        return jnp.einsum("icj,cj->i", values, vector_col, precision=lax.Precision.HIGHEST)

    return lax.map(one_row, (seed_grid, jnp.arange(seed_grid.shape[0], dtype=jnp.int32)))


def lower_sweep(vector_row, factors, lower_inverse, row_span, col_span):
    solved = []
    for sweep_step in range(SWEEPS):
        first_row = sweep_step * row_span
        target = vector_row[first_row : first_row + row_span]
        if sweep_step > 0:
            earlier = jnp.concatenate(solved, axis=0).astype(jnp.bfloat16)
            coupled = jnp.einsum(
                "minj,nj->mi",
                factors[first_row : first_row + row_span, :, : sweep_step * col_span, :],
                earlier,
                preferred_element_type=jnp.float32,
            )
            target = target - lax.psum(coupled, "col")
        mapped = jnp.einsum(
            "cimj,mj->ci",
            lower_inverse[sweep_step],
            target.astype(jnp.bfloat16),
            preferred_element_type=jnp.float32,
        )
        solved.append(lax.psum(mapped, "row"))
    return jnp.concatenate(solved, axis=0)


def upper_sweep(own_rows, factors, upper_inverse, row_span, col_span):
    solved = [None] * SWEEPS
    for sweep_step in reversed(range(SWEEPS)):
        first_row = sweep_step * row_span
        next_col = (sweep_step + 1) * col_span
        own_part = own_rows[first_row : first_row + row_span]
        if sweep_step < SWEEPS - 1:
            later_part = jnp.concatenate(solved[sweep_step + 1 :], axis=0).astype(jnp.bfloat16)
            coupled = jnp.einsum(
                "minj,nj->mi",
                factors[first_row : first_row + row_span, :, next_col:, :],
                later_part,
                preferred_element_type=jnp.float32,
            )
            sent = -coupled
            target = (own_part + lax.psum(sent, "col")).astype(jnp.bfloat16)
        else:
            target = own_part.astype(jnp.bfloat16)
        mapped = jnp.einsum(
            "cimj,mj->ci", upper_inverse[sweep_step], target, preferred_element_type=jnp.float32
        )
        solved[sweep_step] = lax.psum(mapped, "row")
    return jnp.concatenate(solved, axis=0)


def shards(tile_seeds, factors, lower_inverse, upper_inverse, right_side, first_guess):
    n_row = lax.axis_size("row")
    n_col = lax.axis_size("col")
    row_index = lax.axis_index("row")
    col_index = lax.axis_index("col")
    seed_grid = tile_seeds[:, 0, :, 0]
    tile_size = right_side.shape[1]
    row_span = DIAG_ORDER // (tile_size * n_row)
    col_span = DIAG_ORDER // (tile_size * n_col)

    def apply_system(vector_col):
        partial_value = matrix_part(seed_grid, vector_col, row_index, col_index, n_row, n_col)
        return lax.psum(partial_value, "col")

    residual = right_side - apply_system(first_guess)
    initial_norm = jnp.sqrt(lax.psum(jnp.sum(residual * residual), "row"))
    basis_list = [residual / initial_norm]
    directions = []
    hessenberg = jnp.zeros((ITERS + 1, ITERS), jnp.float32)
    for column in range(ITERS):
        lowered = lower_sweep(basis_list[column], factors, lower_inverse, row_span, col_span)
        gathered = lax.all_gather(lowered, "col", axis=1, tiled=True)
        spread = gathered.reshape(-1, n_row, tile_size)
        own_rows = lax.dynamic_index_in_dim(spread, row_index, 1, keepdims=False)
        direction = upper_sweep(own_rows, factors, upper_inverse, row_span, col_span)
        directions.append(direction)
        mapped = apply_system(direction)
        stacked = jnp.stack(basis_list)
        coeffs, squared = lax.psum(
            (jnp.sum(stacked * mapped[None], axis=(1, 2)), jnp.sum(mapped * mapped)), "row"
        )
        mapped = mapped - jnp.sum(coeffs[:, None, None] * stacked, axis=0)
        length = jnp.sqrt(squared - jnp.sum(coeffs * coeffs))
        hessenberg = (
            hessenberg.at[: column + 1, column].set(coeffs).at[column + 1, column].set(length)
        )
        if column + 1 < ITERS:
            basis_list.append(mapped / length)
    normal_matrix = jnp.dot(hessenberg.T, hessenberg, precision=lax.Precision.HIGHEST)
    weights = small_solve(normal_matrix, initial_norm * hessenberg[0])
    solution = first_guess
    for position in range(ITERS):
        solution = solution + weights[position] * directions[position]
    return (solution, hessenberg)


def solution(mesh):
    in_specs = (
        P(None, "row", None, "col"),
        P(None, "row", None, "col"),
        P(None, None, "col", None, "row"),
        P(None, None, "col", None, "row"),
        P(None, "row"),
        P(None, "col"),
    )
    out_specs = (P(None, "col"), P())
    return jax.shard_map(shards, mesh=mesh, in_specs=in_specs, out_specs=out_specs, check_vma=False)
```

profile of v0, /device:TPU:0, one launch (start us, length us, event | category | flops | bytes accessed | tf_op | source)
XLA Modules:
  0.0 2343.3 jit_solution(12727246034049527136)
XLA Ops:
  0.7 321.6 %while.58 = (s32[]{:T(128)}, f32[32,128]{1,0:T(8,128)S(1)}, s32[32,64]{1,0:T(8,128)}, s32[32]{0:T(128)S(1)}, s32[]{:T(128)}, /*index=5*/f32[64,128]{1,0:T(8,128)...) while((s32[]{:T(128)}, f32[32,128]{1,0:T(8,128)S(1)}, ...), condition=%wide.region_1.2_spmd.clone, body=%wide.region_0.1_spmd.clone.sunk | while | flops 33595524 | bytes 8753357 | solution.py:57
  335.6 22.3 psum.372
  413.9 17.8 psum.374
  441.4 19.4 psum.375
  523.5 18.5 fusion.192
  580.5 19.4 psum.379
  669.6 19.4 psum.382
  739.1 17.7 copy.59
  777.8 19.8 psum.386
  797.6 316.5 %while.59 = (s32[]{:T(128)}, f32[32,128]{1,0:T(8,128)S(1)}, s32[32,64]{1,0:T(8,128)}, s32[32]{0:T(128)S(1)}, s32[]{:T(128)}, /*index=5*/f32[64,128]{1,0:T(8,128)...) while((s32[]{:T(128)}, f32[32,128]{1,0:T(8,128)S(1)}, ...), condition=%wide.region_20.21_spmd.clone, body=%wide.region_19.20_spmd.clone.sunk | while | flops 33595524 | bytes 8622257 | solution.py:57
  1124.8 17.8 all-reduce.3
  1148.0 19.4 psum.390
  1209.4 19.5 psum.394
  1268.8 19.4 psum.397
  1330.3 19.4 psum.401
  1381.5 317.2 %while.60 = (s32[]{:T(128)}, f32[32,128]{1,0:T(8,128)S(1)}, s32[32,64]{1,0:T(8,128)}, s32[32]{0:T(128)S(1)}, s32[]{:T(128)}, /*index=5*/f32[64,128]{1,0:T(8,128)...) while((s32[]{:T(128)}, f32[32,128]{1,0:T(8,128)S(1)}, ...), condition=%wide.region_42.43_spmd.clone, body=%wide.region_41.42_spmd.clone.sunk | while | flops 33595524 | bytes 8622257 | solution.py:57
  1709.5 19.8 all-reduce.2
  1763.0 19.3 psum.409
  1795.5 17.8 psum.411
  1827.6 19.3 psum.413
  1884.1 19.3 psum.416
  1948.2 19.5 psum.420
  1967.8 320.8 %while.61 = (s32[]{:T(128)}, f32[32,128]{1,0:T(8,128)S(1)}, s32[32,64]{1,0:T(8,128)}, s32[32]{0:T(128)S(1)}, s32[]{:T(128)}, /*index=5*/f32[64,128]{1,0:T(8,128)...) while((s32[]{:T(128)}, f32[32,128]{1,0:T(8,128)S(1)}, ...), condition=%wide.region_66.67_spmd.clone, body=%wide.region_65.66_spmd.clone.sunk | while | flops 33595524 | bytes 8622257 | solution.py:57
  2299.4 17.8 all-reduce.1
  (1324 shorter events, 1852.1 us)
Async XLA Ops:
  0.7 334.3 %copy-start.2 = (f32[32,128]{1,0:T(8,128)S(1)}, f32[32,128]{1,0:T(8,128)}, u32[]{:S(2)}) copy-start(f32[32,128]{1,0:T(8,128)} %param.30) | copy-start | bytes 49156
  0.7 4.7 copy-start
  10.8 4.7 copy-start
  20.8 4.7 copy-start
  40.9 4.7 copy-start
  50.9 4.7 copy-start
  71.0 4.7 copy-start
  81.1 4.7 copy-start
  101.2 4.7 copy-start
  111.2 4.7 copy-start
  131.3 4.7 copy-start
  141.4 4.7 copy-start
  161.5 4.7 copy-start
  171.5 4.7 copy-start
  191.6 4.7 copy-start
  201.7 4.7 copy-start
  231.8 4.7 copy-start
  241.9 4.7 copy-start
  262.0 4.7 copy-start
  272.0 4.7 copy-start
  292.1 4.7 copy-start
  302.2 4.7 copy-start
  1967.8 357.4 %copy-start.3 = (s32[2]{0:T(128)S(1)}, s32[2]{0:T(128)}, u32[]{:S(2)}) copy-start(s32[2]{0:T(128)} %constant.590.clone.1) | copy-start | bytes 28
  1967.8 374.0 %copy-start.1 = (f32[64,128]{1,0:T(8,128)S(1)}, f32[64,128]{1,0:T(8,128)}, u32[]{:S(2)}) copy-start(f32[64,128]{1,0:T(8,128)} %get-tuple-element.1081) | copy-start | bytes 98308
  (11 other events, 51.4 us)
where the time goes:
time: 2360 us; the launch traced here: 2340 us
  matrix products  827 us (35%)
  blocking collectives  695 us (29%)
  local copies, waits for them, and re-layouts  372 us (16%)
  other arithmetic  341 us (14%)
  loops' own time  92.1 us (4%)
    dot_general x128, matrix products, one_row(): jnp.einsum('icj,cj->i', values, vector_col, precision=lax.Precision.HIGHEST)  681 us
    add x128, other arithmetic, one_row(): values + jnp.where(row_ids[:, None, None] == col_ids[None, :, :], DIAG_SH...  309 us
    psum x12, blocking collectives, upper_sweep(): solved[sweep_step] = lax.psum(mapped, 'row')  221 us
    psum x12, blocking collectives, lower_sweep(): solved.append(lax.psum(mapped, 'row'))  221 us
    another operation x4, loops' own time, matrix_part(): lax.map(one_row, (seed_grid, jnp.arange(seed_grid.shape[0], dtype=jnp.int...  92.1 us
    add x128, local copies, waits for them, and re-layouts, scrambled(): hashed = tile_seed + flat_index * 1640531527  89.3 us
    dynamic_slice x128, local copies, waits for them, and re-layouts, matrix_part(): lax.map(one_row, (seed_grid, jnp.arange(seed_grid.shape[0], dtype=jnp.int...  81.4 us
    slice x6, local copies, waits for them, and re-layouts, upper_sweep(): factors[first_row:first_row + row_span, :, next_col:, :]  74.7 us

commit v1 on v0

--- a/solution.py
+++ b/solution.py
@@ -102,7 +102,7 @@
         mapped = jnp.einsum(
             "cimj,mj->ci", upper_inverse[sweep_step], target, preferred_element_type=jnp.float32
         )
-        solved[sweep_step] = lax.psum(mapped, "row")
+        solved[sweep_step] = jnp.sum(lax.all_gather(mapped, "row"), axis=0)
     return jnp.concatenate(solved, axis=0)
 
 

time: 2360 us -> 2480 us (1.051)
  blocking collectives: 695 us -> 829 us
    all_gather x0 -> x12, blocking collectives: none -> 367 us  [upper_sweep(): solved[sweep_step] = jnp.sum(lax.all_gather(mapped, 'row'), axis=0)]
    psum x12 -> x0, blocking collectives: 221 us -> none  [upper_sweep(): solved[sweep_step] = lax.psum(mapped, 'row')]
where the time goes in v1:
time: 2480 us; the launch traced here: 2470 us
  blocking collectives  829 us (33%)
  matrix products  827 us (33%)
  local copies, waits for them, and re-layouts  367 us (15%)
  other arithmetic  341 us (14%)
  loops' own time  84.9 us (3%)
    dot_general x128, matrix products, one_row(): jnp.einsum('icj,cj->i', values, vector_col, precision=lax.Precision.HIGHEST)  681 us
    all_gather x12, blocking collectives, upper_sweep(): solved[sweep_step] = jnp.sum(lax.all_gather(mapped, 'row'), axis=0)  367 us
    add x128, other arithmetic, one_row(): values + jnp.where(row_ids[:, None, None] == col_ids[None, :, :], DIAG_SH...  309 us
    psum x12, blocking collectives, lower_sweep(): solved.append(lax.psum(mapped, 'row'))  221 us
    add x128, local copies, waits for them, and re-layouts, scrambled(): hashed = tile_seed + flat_index * 1640531527  89.3 us
    another operation x4, loops' own time, matrix_part(): lax.map(one_row, (seed_grid, jnp.arange(seed_grid.shape[0], dtype=jnp.int...  84.9 us
    dynamic_slice x128, local copies, waits for them, and re-layouts, matrix_part(): lax.map(one_row, (seed_grid, jnp.arange(seed_grid.shape[0], dtype=jnp.int...  76.8 us
    slice x6, local copies, waits for them, and re-layouts, upper_sweep(): factors[first_row:first_row + row_span, :, next_col:, :]  74.7 us

profile of v1, /device:TPU:0, one launch (start us, length us, event | category | flops | bytes accessed | tf_op | source)
XLA Modules:
  0.0 2465.3 jit_solution(8285756175983078)
XLA Ops:
  0.7 321.6 %while.58 = (s32[]{:T(128)}, f32[32,128]{1,0:T(8,128)S(1)}, s32[32,64]{1,0:T(8,128)}, s32[32]{0:T(128)S(1)}, s32[]{:T(128)}, /*index=5*/f32[64,128]{1,0:T(8,128)...) while((s32[]{:T(128)}, f32[32,128]{1,0:T(8,128)S(1)}, ...), condition=%wide.region_1.2_spmd.clone, body=%wide.region_0.1_spmd.clone.sunk | while | flops 33595524 | bytes 8753357 | solution.py:57
  335.6 22.3 psum.288
  429.4 19.4 psum.291
  568.7 19.4 psum.295
  615.3 30.5 %all-gather = f32[128,128]{1,0:T(8,128)S(1)} all-gather(f32[16,128]{1,0:T(8,128)S(1)} %bitcast.441), channel_id=2, replica_groups=mesh['row'=8,'col'=4] {'row'}, dimensions={0}, use_global_device_ids=true | all-gather | bytes 73728 | tf_op jit(solution)/shard_map/all_gather | solution.py:105
  670.9 30.5 %all-gather.1 = f32[128,128]{1,0:T(8,128)S(1)} all-gather(f32[16,128]{1,0:T(8,128)S(1)} %bitcast.435), channel_id=3, replica_groups=mesh['row'=8,'col'=4] {'row'}, dimensions={0}, use_global_device_ids=true | all-gather | bytes 73728 | tf_op jit(solution)/shard_map/all_gather | solution.py:105
  734.3 30.5 %all-gather.2 = f32[128,128]{1,0:T(8,128)S(1)} all-gather(f32[16,128]{1,0:T(8,128)S(1)} %bitcast.436), channel_id=4, replica_groups=mesh['row'=8,'col'=4] {'row'}, dimensions={0}, use_global_device_ids=true | all-gather | bytes 73728 | tf_op jit(solution)/shard_map/all_gather | solution.py:105
  803.4 30.9 %all-gather.3 = f32[128,128]{1,0:T(8,128)S(1)} all-gather(f32[16,128]{1,0:T(8,128)S(1)} %bitcast.437), channel_id=5, replica_groups=mesh['row'=8,'col'=4] {'row'}, dimensions={0}, use_global_device_ids=true | all-gather | bytes 73728 | tf_op jit(solution)/shard_map/all_gather | solution.py:105
  834.4 312.8 %while.59 = (s32[]{:T(128)}, f32[32,128]{1,0:T(8,128)S(1)}, s32[32,64]{1,0:T(8,128)}, s32[32]{0:T(128)S(1)}, s32[]{:T(128)}, /*index=5*/f32[64,128]{1,0:T(8,128)...) while((s32[]{:T(128)}, f32[32,128]{1,0:T(8,128)S(1)}, ...), condition=%wide.region_20.21_spmd.clone, body=%wide.region_19.20_spmd.clone.sunk | while | flops 33595524 | bytes 8622257 | solution.py:57
  1180.9 19.4 psum.302
  1242.3 19.5 psum.306
  1301.7 30.5 %all-gather.4 = f32[128,128]{1,0:T(8,128)S(1)} all-gather(f32[16,128]{1,0:T(8,128)S(1)} %bitcast.442), channel_id=6, replica_groups=mesh['row'=8,'col'=4] {'row'}, dimensions={0}, use_global_device_ids=true | all-gather | bytes 73728 | tf_op jit(solution)/shard_map/all_gather | solution.py:105
  1343.8 30.5 %all-gather.5 = f32[128,128]{1,0:T(8,128)S(1)} all-gather(f32[16,128]{1,0:T(8,128)S(1)} %bitcast.438), channel_id=7, replica_groups=mesh['row'=8,'col'=4] {'row'}, dimensions={0}, use_global_device_ids=true | all-gather | bytes 73728 | tf_op jit(solution)/shard_map/all_gather | solution.py:105
  1387.5 30.5 %all-gather.6 = f32[128,128]{1,0:T(8,128)S(1)} all-gather(f32[16,128]{1,0:T(8,128)S(1)} %bitcast.439), channel_id=8, replica_groups=mesh['row'=8,'col'=4] {'row'}, dimensions={0}, use_global_device_ids=true | all-gather | bytes 73728 | tf_op jit(solution)/shard_map/all_gather | solution.py:105
  1432.3 30.7 %all-gather.7 = f32[128,128]{1,0:T(8,128)S(1)} all-gather(f32[16,128]{1,0:T(8,128)S(1)} %bitcast.440), channel_id=9, replica_groups=mesh['row'=8,'col'=4] {'row'}, dimensions={0}, use_global_device_ids=true | all-gather | bytes 73728 | tf_op jit(solution)/shard_map/all_gather | solution.py:105
  1463.1 316.0 %while.60 = (s32[]{:T(128)}, f32[32,128]{1,0:T(8,128)S(1)}, s32[32,64]{1,0:T(8,128)}, s32[32]{0:T(128)S(1)}, s32[]{:T(128)}, /*index=5*/f32[64,128]{1,0:T(8,128)...) while((s32[]{:T(128)}, f32[32,128]{1,0:T(8,128)S(1)}, ...), condition=%wide.region_42.43_spmd.clone, body=%wide.region_41.42_spmd.clone.sunk | while | flops 33595524 | bytes 8622257 | solution.py:57
  1789.9 19.7 all-reduce.2
  1843.3 19.3 psum.317
  1907.8 19.3 psum.321
  1935.4 30.5 %all-gather.8 = f32[128,128]{1,0:T(8,128)S(1)} all-gather(f32[16,128]{1,0:T(8,128)S(1)} %bitcast.431), channel_id=10, replica_groups=mesh['row'=8,'col'=4] {'row'}, dimensions={0}, use_global_device_ids=true | all-gather | bytes 73728 | tf_op jit(solution)/shard_map/all_gather | solution.py:105
  1977.4 30.5 %all-gather.9 = f32[128,128]{1,0:T(8,128)S(1)} all-gather(f32[16,128]{1,0:T(8,128)S(1)} %bitcast.432), channel_id=11, replica_groups=mesh['row'=8,'col'=4] {'row'}, dimensions={0}, use_global_device_ids=true | all-gather | bytes 73728 | tf_op jit(solution)/shard_map/all_gather | solution.py:105
  2021.2 30.5 %all-gather.10 = f32[128,128]{1,0:T(8,128)S(1)} all-gather(f32[16,128]{1,0:T(8,128)S(1)} %bitcast.433), channel_id=12, replica_groups=mesh['row'=8,'col'=4] {'row'}, dimensions={0}, use_global_device_ids=true | all-gather | bytes 73728 | tf_op jit(solution)/shard_map/all_gather | solution.py:105
  2066.0 30.7 %all-gather.11 = f32[128,128]{1,0:T(8,128)S(1)} all-gather(f32[16,128]{1,0:T(8,128)S(1)} %bitcast.434), channel_id=13, replica_groups=mesh['row'=8,'col'=4] {'row'}, dimensions={0}, use_global_device_ids=true | all-gather | bytes 73728 | tf_op jit(solution)/shard_map/all_gather | solution.py:105
  2096.7 313.8 %while.61 = (s32[]{:T(128)}, f32[32,128]{1,0:T(8,128)S(1)}, s32[32,64]{1,0:T(8,128)}, s32[32]{0:T(128)S(1)}, s32[]{:T(128)}, /*index=5*/f32[64,128]{1,0:T(8,128)...) while((s32[]{:T(128)}, f32[32,128]{1,0:T(8,128)S(1)}, ...), condition=%wide.region_66.67_spmd.clone, body=%wide.region_65.66_spmd.clone.sunk | while | flops 33595524 | bytes 8622257 | solution.py:57
  (1327 shorter events, 1838.6 us)
Async XLA Ops:
  0.7 334.3 %copy-start.2 = (f32[32,128]{1,0:T(8,128)S(1)}, f32[32,128]{1,0:T(8,128)}, u32[]{:S(2)}) copy-start(f32[32,128]{1,0:T(8,128)} %param.30) | copy-start | bytes 49156
  0.7 4.7 copy-start
  10.8 4.7 copy-start
  30.9 4.7 copy-start
  40.9 4.7 copy-start
  61.0 4.7 copy-start
  71.0 4.7 copy-start
  91.1 4.7 copy-start
  101.2 4.7 copy-start
  121.3 4.7 copy-start
  131.3 4.7 copy-start
  151.4 4.7 copy-start
  161.5 4.7 copy-start
  191.6 4.7 copy-start
  201.7 4.7 copy-start
  221.8 4.7 copy-start
  231.8 4.7 copy-start
  251.9 4.7 copy-start
  262.0 4.7 copy-start
  282.1 4.7 copy-start
  292.1 4.7 copy-start
  312.2 4.7 copy-start
  2096.7 350.5 %copy-start.3 = (s32[2]{0:T(128)S(1)}, s32[2]{0:T(128)}, u32[]{:S(2)}) copy-start(s32[2]{0:T(128)} %constant.590.clone.1) | copy-start | bytes 28
  2096.7 367.1 %copy-start.1 = (f32[64,128]{1,0:T(8,128)S(1)}, f32[64,128]{1,0:T(8,128)}, u32[]{:S(2)}) copy-start(f32[64,128]{1,0:T(8,128)} %get-tuple-element.1080) | copy-start | bytes 98308
  (11 other events, 51.4 us)
